TPU v7x, 32 devices: a whole 2x2x4 slice. The times are simulated.
32 devices in a mesh: section: 4 (over z), rows: 8 (over y, x, core).
Axes of the slice: x: 2, y: 2, z: 4, core: 2. Of those that a mesh axis runs over, the one named last changes fastest.
Arguments:
- features: bfloat16 [1024, 1536], P('rows'), may hold values from -6 to 6
- ages: int32 [1024], P('rows'), may hold values from 0 to 15
- age_table: bfloat16 [16, 1536], replicated, may hold values from -3 to 3
- returns: float32 [1024], P('rows'), may hold values from -6 to 6
- owners: int32 [1024, 1], P('rows'), may hold values from 0 to 7; in each aligned block of 128 rows (0 to 127, 128 to 255, ...) at most 32 rows name the same one
- slots: int32 [1024], P('rows'), may hold values from 0 to 4095
- norm_gain: float32 [4, 1536], P('section'), may hold values from 0.1 to 1.9
- w_gate: bfloat16 [4, 1536, 8960], P('section', None, 'rows'), may hold values from -0.15625 to 0.15625
- w_up: bfloat16 [4, 1536, 8960], P('section', None, 'rows'), may hold values from -0.15625 to 0.15625
- w_down: bfloat16 [4, 8960, 1536], P('section', 'rows'), may hold values from -0.0625 to 0.0625
- final_gain: float32 [1536], replicated, may hold values from 0.1 to 1.9
- reward_head: float32 [1536], replicated, may hold values from -0.15625 to 0.15625
- old_priority: float32 [32768], P('rows'), may hold values from 0.05 to 2
Outputs:
- rewards: float32 [1024], P(('rows', 'section'))
- weights: float32 [32768], P(('rows', 'section'))
Inputs may be any that keep to these rules, and one draw needn't show every extreme that they name: `owners`: among the rows of one device at most 32 name the same owner; in every draw some owner is named by exactly 32 rows of some device.
All inputs are finite; a program needn't handle non-finite values.
Results may differ from a plain program's by a relative error of at most 0.04.
Values may be sent and summed in bfloat16 or wider, within the bound.
A program may use at most 64 MiB of HBM per device.

v0:
```python
import jax
import jax.numpy as jnp
from jax import lax
from jax.sharding import PartitionSpec as P

MICRO = 8
CAP = 32


def shifted(value, axis, steps):
    count = lax.axis_size(axis)
    first, last = (max(0, -steps), min(count, count - steps))
    return lax.ppermute(value, axis, [(source, source + steps) for source in range(first, last)])


def spread(value, axis, source):
    kept = jnp.where(lax.axis_index(axis) == source, value, 0).astype(value.dtype)
    return lax.psum(kept, axis)


def scaled_norm(values, gain):
    return values * lax.rsqrt(jnp.mean(values * values, axis=-1, keepdims=True) + 1e-06) * gain


def on_device(
    features,
    ages,
    age_table,
    returns,
    owners,
    slots,
    norm_gain,
    w_gate,
    w_up,
    w_down,
    final_gain,
    reward_head,
    old_priority,
):
    sections = lax.axis_size("section")
    section_now = lax.axis_index("section")
    groups = lax.axis_size("rows")
    rows_here = features.shape[0]
    block = rows_here // MICRO
    width = features.shape[1]
    table_size = old_priority.shape[0]
    onehot = (ages[:, None] == jnp.arange(age_table.shape[0])[None, :]).astype(jnp.bfloat16)
    entry = (
        features.astype(jnp.float32)
        + jnp.dot(onehot, age_table, preferred_element_type=jnp.float32)
    ).astype(jnp.bfloat16)

    def layer_split(state, layer):
        wide = state.astype(jnp.float32)
        normed = scaled_norm(wide, norm_gain[layer]).astype(jnp.bfloat16)
        piece = lax.all_gather(normed, "rows", axis=0, tiled=True)
        gate = jnp.dot(piece, w_gate[layer], preferred_element_type=jnp.float32)
        upper = jnp.dot(piece, w_up[layer], preferred_element_type=jnp.float32)
        hidden = (jax.nn.silu(gate) * upper).astype(jnp.bfloat16)
        summed = lax.psum_scatter(
            jnp.dot(hidden, w_down[layer], preferred_element_type=jnp.float32).astype(jnp.bfloat16),
            "rows",
            scatter_dimension=0,
            tiled=True,
        ).astype(jnp.float32)
        return (wide + summed).astype(jnp.bfloat16)

    def tick(carry, step):
        current, collected = carry
        pick = jnp.minimum(step, MICRO - 1)
        block_in = lax.dynamic_slice_in_dim(entry, pick * block, block, 0)
        state = jnp.where(section_now == 0, block_in, current)
        state = layer_split(state, 0)
        finished_block = step - (sections - 1)
        valid = jnp.logical_and(section_now == sections - 1, finished_block >= 0)
        placed = lax.dynamic_update_slice_in_dim(
            collected, state, jnp.maximum(finished_block, 0) * block, 0
        )
        collected = jnp.where(valid, placed, collected)
        current = shifted(state, "section", 1)
        return ((current, collected), None)

    start_state = jnp.zeros((block, width), jnp.bfloat16)
    start_rows = jnp.zeros((rows_here, width), jnp.bfloat16)
    (unused_state, collected), unused_out = lax.scan(
        tick, (start_state, start_rows), jnp.arange(MICRO + sections - 1)
    )
    finished = scaled_norm(collected.astype(jnp.float32), final_gain)
    rewards_here = jnp.sum(finished * reward_head, axis=-1)
    rewards_here = spread(rewards_here, "section", sections - 1)
    priority = jnp.exp(0.6 * jnp.log(jnp.abs(rewards_here - returns) + 0.05))
    owner = owners[:, 0]
    entries = jnp.arange(table_size)
    owner_hits = (owner[:, None] == jnp.arange(groups)[None, :]).astype(jnp.int32)
    rank = jnp.sum(jnp.cumsum(owner_hits, axis=0) * owner_hits, axis=1) - 1
    position = owner * CAP + rank
    send_values = jnp.zeros((groups * CAP,), jnp.float32).at[position].set(priority)
    send_places = (
        jnp.full((groups * CAP,), -1.0, jnp.float32).at[position].set(slots.astype(jnp.float32))
    )
    got_values, got_places = (
        lax.all_to_all(send_values, "rows", split_axis=0, concat_axis=0, tiled=True),
        lax.all_to_all(send_places, "rows", split_axis=0, concat_axis=0, tiled=True),
    )
    match = got_places[:, None] == entries[None, :].astype(jnp.float32)
    best = jnp.max(jnp.where(match, got_values[:, None], 0.0), axis=0)
    refreshed = jnp.where(best > 0.0, best, old_priority)
    total = lax.psum(jnp.sum(refreshed), "rows")
    weights = refreshed * (table_size * groups / total)
    reward_part = rows_here // sections
    weight_part = table_size // sections
    rewards_out = lax.dynamic_slice_in_dim(rewards_here, section_now * reward_part, reward_part, 0)
    weights_out = lax.dynamic_slice_in_dim(weights, section_now * weight_part, weight_part, 0)
    return (rewards_out, weights_out)


def solution(mesh):
    placed = (
        P("rows", None),
        P("rows"),
        P(),
        P("rows"),
        P("rows", None),
        P("rows"),
        P("section", None),
        P("section", None, "rows"),
        P("section", None, "rows"),
        P("section", "rows", None),
        P(),
        P(),
        P("rows"),
    )
    return jax.shard_map(
        on_device,
        mesh=mesh,
        in_specs=placed,
        out_specs=(P(("rows", "section")), P(("rows", "section"))),
        check_vma=False,
    )
```

profile of v0, /device:TPU:0, one launch (start us, length us, event | category | flops | bytes accessed | tf_op | source)
XLA Modules:
  0.0 745.7 jit_solution(18402133200371341177)
XLA Ops:
  9.4 683.1 %while.14 = (s32[]{:T(128)}, bf16[16,1536]{1,0:T(8,128)(2,1)S(1)}, bf16[128,1536]{1,0:T(8,128)(2,1)S(1)}, pred[]{:T(512)}, s32[11]{0:T(128)S(1)}, /*index=5*/bf1...) while((s32[]{:T(128)}, bf16[16,1536]{1,0:T(8,128)(2,1)S(1)}, ...), condition=%wide.region_3.4_spmd, body=%wide.region_0.3_spmd.sunk | while | flops 1322582016 | bytes 15125155 | solution.py:85
  11.8 11.1 %all_gather.7 = bf16[128,1536]{1,0:T(8,128)(2,1)S(1)} all-gather(bf16[16,1536]{1,0:T(8,128)(2,1)S(1)} %fusion.60), channel_id=1, replica_groups=mesh['section'=4,'rows'=8] {'rows'}, dimensions={0}, use_global_device_ids=true | all-gather | bytes 442368 | tf_op jit(solution)/shard_map/while/body/eval_jaxpr/all_gather | solution.py:56
  25.9 6.3 fusion.62
  32.9 33.7 %reduce-scatter.2.cloned.1.call-done = bf16[16,1536]{1,0:T(8,128)(2,1)} async-done(((bf16[128,1536]{1,0:T(8,128)(2,1)}), bf16[16,1536]{1,0:T(8,128)(2,1)}) %reduce-scatter.2.cloned.1.call-update) | async-done | bytes 49168 | tf_op jit(solution)/shard_map/while/body/eval_jaxpr/reduce_scatter | solution.py:60
  67.3 3.4 collective-permute-start
  74.8 9.5 %all_gather.7 = bf16[128,1536]{1,0:T(8,128)(2,1)S(1)} all-gather(bf16[16,1536]{1,0:T(8,128)(2,1)S(1)} %fusion.60), channel_id=1, replica_groups=mesh['section'=4,'rows'=8] {'rows'}, dimensions={0}, use_global_device_ids=true | all-gather | bytes 442368 | tf_op jit(solution)/shard_map/while/body/eval_jaxpr/all_gather | solution.py:56
  87.3 6.3 fusion.62
  94.3 34.2 %reduce-scatter.2.cloned.1.call-done = bf16[16,1536]{1,0:T(8,128)(2,1)} async-done(((bf16[128,1536]{1,0:T(8,128)(2,1)}), bf16[16,1536]{1,0:T(8,128)(2,1)}) %reduce-scatter.2.cloned.1.call-update) | async-done | bytes 49168 | tf_op jit(solution)/shard_map/while/body/eval_jaxpr/reduce_scatter | solution.py:60
  129.3 3.4 collective-permute-start
  136.8 9.5 %all_gather.7 = bf16[128,1536]{1,0:T(8,128)(2,1)S(1)} all-gather(bf16[16,1536]{1,0:T(8,128)(2,1)S(1)} %fusion.60), channel_id=1, replica_groups=mesh['section'=4,'rows'=8] {'rows'}, dimensions={0}, use_global_device_ids=true | all-gather | bytes 442368 | tf_op jit(solution)/shard_map/while/body/eval_jaxpr/all_gather | solution.py:56
  149.3 6.3 fusion.62
  156.3 34.2 %reduce-scatter.2.cloned.1.call-done = bf16[16,1536]{1,0:T(8,128)(2,1)} async-done(((bf16[128,1536]{1,0:T(8,128)(2,1)}), bf16[16,1536]{1,0:T(8,128)(2,1)}) %reduce-scatter.2.cloned.1.call-update) | async-done | bytes 49168 | tf_op jit(solution)/shard_map/while/body/eval_jaxpr/reduce_scatter | solution.py:60
  191.3 3.4 collective-permute-start
  198.8 9.5 %all_gather.7 = bf16[128,1536]{1,0:T(8,128)(2,1)S(1)} all-gather(bf16[16,1536]{1,0:T(8,128)(2,1)S(1)} %fusion.60), channel_id=1, replica_groups=mesh['section'=4,'rows'=8] {'rows'}, dimensions={0}, use_global_device_ids=true | all-gather | bytes 442368 | tf_op jit(solution)/shard_map/while/body/eval_jaxpr/all_gather | solution.py:56
  211.3 6.3 fusion.62
  218.3 34.2 %reduce-scatter.2.cloned.1.call-done = bf16[16,1536]{1,0:T(8,128)(2,1)} async-done(((bf16[128,1536]{1,0:T(8,128)(2,1)}), bf16[16,1536]{1,0:T(8,128)(2,1)}) %reduce-scatter.2.cloned.1.call-update) | async-done | bytes 49168 | tf_op jit(solution)/shard_map/while/body/eval_jaxpr/reduce_scatter | solution.py:60
  253.4 3.4 collective-permute-start
  260.8 9.5 %all_gather.7 = bf16[128,1536]{1,0:T(8,128)(2,1)S(1)} all-gather(bf16[16,1536]{1,0:T(8,128)(2,1)S(1)} %fusion.60), channel_id=1, replica_groups=mesh['section'=4,'rows'=8] {'rows'}, dimensions={0}, use_global_device_ids=true | all-gather | bytes 442368 | tf_op jit(solution)/shard_map/while/body/eval_jaxpr/all_gather | solution.py:56
  273.3 6.3 fusion.62
  280.3 34.2 %reduce-scatter.2.cloned.1.call-done = bf16[16,1536]{1,0:T(8,128)(2,1)} async-done(((bf16[128,1536]{1,0:T(8,128)(2,1)}), bf16[16,1536]{1,0:T(8,128)(2,1)}) %reduce-scatter.2.cloned.1.call-update) | async-done | bytes 49168 | tf_op jit(solution)/shard_map/while/body/eval_jaxpr/reduce_scatter | solution.py:60
  315.4 3.4 collective-permute-start
  322.8 9.5 %all_gather.7 = bf16[128,1536]{1,0:T(8,128)(2,1)S(1)} all-gather(bf16[16,1536]{1,0:T(8,128)(2,1)S(1)} %fusion.60), channel_id=1, replica_groups=mesh['section'=4,'rows'=8] {'rows'}, dimensions={0}, use_global_device_ids=true | all-gather | bytes 442368 | tf_op jit(solution)/shard_map/while/body/eval_jaxpr/all_gather | solution.py:56
  335.4 6.3 fusion.62
  342.3 34.2 %reduce-scatter.2.cloned.1.call-done = bf16[16,1536]{1,0:T(8,128)(2,1)} async-done(((bf16[128,1536]{1,0:T(8,128)(2,1)}), bf16[16,1536]{1,0:T(8,128)(2,1)}) %reduce-scatter.2.cloned.1.call-update) | async-done | bytes 49168 | tf_op jit(solution)/shard_map/while/body/eval_jaxpr/reduce_scatter | solution.py:60
  377.4 3.4 collective-permute-start
  384.8 9.5 %all_gather.7 = bf16[128,1536]{1,0:T(8,128)(2,1)S(1)} all-gather(bf16[16,1536]{1,0:T(8,128)(2,1)S(1)} %fusion.60), channel_id=1, replica_groups=mesh['section'=4,'rows'=8] {'rows'}, dimensions={0}, use_global_device_ids=true | all-gather | bytes 442368 | tf_op jit(solution)/shard_map/while/body/eval_jaxpr/all_gather | solution.py:56
  397.4 6.3 fusion.62
  404.4 34.2 %reduce-scatter.2.cloned.1.call-done = bf16[16,1536]{1,0:T(8,128)(2,1)} async-done(((bf16[128,1536]{1,0:T(8,128)(2,1)}), bf16[16,1536]{1,0:T(8,128)(2,1)}) %reduce-scatter.2.cloned.1.call-update) | async-done | bytes 49168 | tf_op jit(solution)/shard_map/while/body/eval_jaxpr/reduce_scatter | solution.py:60
  439.4 3.4 collective-permute-start
  446.8 9.6 %all_gather.7 = bf16[128,1536]{1,0:T(8,128)(2,1)S(1)} all-gather(bf16[16,1536]{1,0:T(8,128)(2,1)S(1)} %fusion.60), channel_id=1, replica_groups=mesh['section'=4,'rows'=8] {'rows'}, dimensions={0}, use_global_device_ids=true | all-gather | bytes 442368 | tf_op jit(solution)/shard_map/while/body/eval_jaxpr/all_gather | solution.py:56
  459.4 6.3 fusion.62
  466.4 34.2 %reduce-scatter.2.cloned.1.call-done = bf16[16,1536]{1,0:T(8,128)(2,1)} async-done(((bf16[128,1536]{1,0:T(8,128)(2,1)}), bf16[16,1536]{1,0:T(8,128)(2,1)}) %reduce-scatter.2.cloned.1.call-update) | async-done | bytes 49168 | tf_op jit(solution)/shard_map/while/body/eval_jaxpr/reduce_scatter | solution.py:60
  501.4 3.4 collective-permute-start
  508.8 9.5 %all_gather.7 = bf16[128,1536]{1,0:T(8,128)(2,1)S(1)} all-gather(bf16[16,1536]{1,0:T(8,128)(2,1)S(1)} %fusion.60), channel_id=1, replica_groups=mesh['section'=4,'rows'=8] {'rows'}, dimensions={0}, use_global_device_ids=true | all-gather | bytes 442368 | tf_op jit(solution)/shard_map/while/body/eval_jaxpr/all_gather | solution.py:56
  521.4 6.3 fusion.62
  528.4 34.2 %reduce-scatter.2.cloned.1.call-done = bf16[16,1536]{1,0:T(8,128)(2,1)} async-done(((bf16[128,1536]{1,0:T(8,128)(2,1)}), bf16[16,1536]{1,0:T(8,128)(2,1)}) %reduce-scatter.2.cloned.1.call-update) | async-done | bytes 49168 | tf_op jit(solution)/shard_map/while/body/eval_jaxpr/reduce_scatter | solution.py:60
  563.4 3.4 collective-permute-start
  570.8 9.5 %all_gather.7 = bf16[128,1536]{1,0:T(8,128)(2,1)S(1)} all-gather(bf16[16,1536]{1,0:T(8,128)(2,1)S(1)} %fusion.60), channel_id=1, replica_groups=mesh['section'=4,'rows'=8] {'rows'}, dimensions={0}, use_global_device_ids=true | all-gather | bytes 442368 | tf_op jit(solution)/shard_map/while/body/eval_jaxpr/all_gather | solution.py:56
  583.4 6.3 fusion.62
  590.4 34.2 %reduce-scatter.2.cloned.1.call-done = bf16[16,1536]{1,0:T(8,128)(2,1)} async-done(((bf16[128,1536]{1,0:T(8,128)(2,1)}), bf16[16,1536]{1,0:T(8,128)(2,1)}) %reduce-scatter.2.cloned.1.call-update) | async-done | bytes 49168 | tf_op jit(solution)/shard_map/while/body/eval_jaxpr/reduce_scatter | solution.py:60
  625.4 3.4 collective-permute-start
  632.8 9.5 %all_gather.7 = bf16[128,1536]{1,0:T(8,128)(2,1)S(1)} all-gather(bf16[16,1536]{1,0:T(8,128)(2,1)S(1)} %fusion.60), channel_id=1, replica_groups=mesh['section'=4,'rows'=8] {'rows'}, dimensions={0}, use_global_device_ids=true | all-gather | bytes 442368 | tf_op jit(solution)/shard_map/while/body/eval_jaxpr/all_gather | solution.py:56
  645.4 6.3 fusion.62
  652.4 34.2 %reduce-scatter.2.cloned.1.call-done = bf16[16,1536]{1,0:T(8,128)(2,1)} async-done(((bf16[128,1536]{1,0:T(8,128)(2,1)}), bf16[16,1536]{1,0:T(8,128)(2,1)}) %reduce-scatter.2.cloned.1.call-update) | async-done | bytes 49168 | tf_op jit(solution)/shard_map/while/body/eval_jaxpr/reduce_scatter | solution.py:60
  687.4 3.4 collective-permute-start
  693.0 12.5 %psum.14 = f32[128]{0:T(128)S(1)} all-reduce(f32[128]{0:T(128)S(1)} %broadcast_select_fusion), channel_id=1, replica_groups=mesh['section'=4,'rows'=8] {'section'}, use_global_device_ids=true, to_apply=%region_6.7 | all-reduce | flops 128 | bytes 1024 | tf_op jit(solution)/shard_map/psum | solution.py:18
  715.5 3.3 all-to-all-start
  725.4 12.4 %psum.15 = f32[]{:T(128)} all-reduce(f32[]{:T(128)} %get-tuple-element.161), channel_id=1, replica_groups=mesh['section'=4,'rows'=8] {'rows'}, use_global_device_ids=true, to_apply=%region_13.14 | all-reduce | flops 1 | bytes 8 | tf_op jit(solution)/shard_map/psum | solution.py:108
  (155 shorter events, 98.7 us)
Async XLA Ops:
  7.2 0.8 copy-start
  9.3 683.4 %copy-start.2 = (f32[1536]{0:T(1024)S(1)}, f32[1536]{0:T(1024)}, u32[]{:S(2)}) copy-start(f32[1536]{0:T(1024)} %param.26) | copy-start | bytes 18436
  9.4 683.3 %copy-start.3 = (f32[1536]{0:T(1024)S(1)}, f32[1536]{0:T(1024)}, u32[]{:S(2)}) copy-start(f32[1536]{0:T(1024)} %param.25) | copy-start | bytes 18436
  9.4 696.2 %copy-start.4 = (s32[128,1]{0,1:T(1,128)S(1)}, s32[128,1]{0,1:T(1,128)}, u32[]{:S(2)}) copy-start(s32[128,1]{0,1:T(1,128)} %param.19) | copy-start | bytes 1540
  9.4 696.6 %copy-start.5 = (f32[128]{0:T(128)S(1)}, f32[128]{0:T(128)}, u32[]{:S(2)}) copy-start(f32[128]{0:T(128)} %param.18) | copy-start | bytes 1540
  9.4 701.6 %copy-start.6 = (s32[128]{0:T(128)S(1)}, s32[128]{0:T(128)}, u32[]{:S(2)}) copy-start(s32[128]{0:T(128)} %param.20) | copy-start | bytes 1540
  9.4 715.4 %copy-start.1 = (f32[4096]{0:T(1024)S(1)}, f32[4096]{0:T(1024)}, u32[]{:S(2)}) copy-start(f32[4096]{0:T(1024)} %param.27) | copy-start | bytes 49156
  9.4 57.1 %reduce-scatter.2.cloned.1.call-start = ((), (), s32[]{:S(2)}) async-start(), calls=%async_computation.3 | async-start | bytes 442368 | tf_op jit(solution)/shard_map/while/body/eval_jaxpr/reduce_scatter | solution.py:60
  67.3 5.1 collective-permute-start
  72.5 56.0 %reduce-scatter.2.cloned.1.call-start = ((), (), s32[]{:S(2)}) async-start(), calls=%async_computation.3 | async-start | bytes 442368 | tf_op jit(solution)/shard_map/while/body/eval_jaxpr/reduce_scatter | solution.py:60
  129.3 5.1 collective-permute-start
  134.5 56.1 %reduce-scatter.2.cloned.1.call-start = ((), (), s32[]{:S(2)}) async-start(), calls=%async_computation.3 | async-start | bytes 442368 | tf_op jit(solution)/shard_map/while/body/eval_jaxpr/reduce_scatter | solution.py:60
  191.3 5.1 collective-permute-start
  196.5 56.1 %reduce-scatter.2.cloned.1.call-start = ((), (), s32[]{:S(2)}) async-start(), calls=%async_computation.3 | async-start | bytes 442368 | tf_op jit(solution)/shard_map/while/body/eval_jaxpr/reduce_scatter | solution.py:60
  253.4 5.1 collective-permute-start
  258.5 56.0 %reduce-scatter.2.cloned.1.call-start = ((), (), s32[]{:S(2)}) async-start(), calls=%async_computation.3 | async-start | bytes 442368 | tf_op jit(solution)/shard_map/while/body/eval_jaxpr/reduce_scatter | solution.py:60
  315.4 5.1 collective-permute-start
  320.5 56.1 %reduce-scatter.2.cloned.1.call-start = ((), (), s32[]{:S(2)}) async-start(), calls=%async_computation.3 | async-start | bytes 442368 | tf_op jit(solution)/shard_map/while/body/eval_jaxpr/reduce_scatter | solution.py:60
  377.4 5.1 collective-permute-start
  382.5 56.0 %reduce-scatter.2.cloned.1.call-start = ((), (), s32[]{:S(2)}) async-start(), calls=%async_computation.3 | async-start | bytes 442368 | tf_op jit(solution)/shard_map/while/body/eval_jaxpr/reduce_scatter | solution.py:60
  439.4 5.1 collective-permute-start
  444.5 56.1 %reduce-scatter.2.cloned.1.call-start = ((), (), s32[]{:S(2)}) async-start(), calls=%async_computation.3 | async-start | bytes 442368 | tf_op jit(solution)/shard_map/while/body/eval_jaxpr/reduce_scatter | solution.py:60
  501.4 5.1 collective-permute-start
  506.6 56.0 %reduce-scatter.2.cloned.1.call-start = ((), (), s32[]{:S(2)}) async-start(), calls=%async_computation.3 | async-start | bytes 442368 | tf_op jit(solution)/shard_map/while/body/eval_jaxpr/reduce_scatter | solution.py:60
  563.4 5.1 collective-permute-start
  568.6 56.0 %reduce-scatter.2.cloned.1.call-start = ((), (), s32[]{:S(2)}) async-start(), calls=%async_computation.3 | async-start | bytes 442368 | tf_op jit(solution)/shard_map/while/body/eval_jaxpr/reduce_scatter | solution.py:60
  625.4 5.1 collective-permute-start
  630.6 56.0 %reduce-scatter.2.cloned.1.call-start = ((), (), s32[]{:S(2)}) async-start(), calls=%async_computation.3 | async-start | bytes 442368 | tf_op jit(solution)/shard_map/while/body/eval_jaxpr/reduce_scatter | solution.py:60
  687.4 5.1 collective-permute-start
  707.7 7.9 %all-to-all-start.1 = ((f32[8,32,1]{1,2,0:T(1,128)}), f32[8,32,1]{1,2,0:T(1,128)S(1)}, u32[]{:S(2)}, u32[]{:S(2)}) async-start(f32[8,32,1]{1,2,0:T(1,128)} %bitcast.10), calls=%async_computation.2 | async-start | bytes 8192 | tf_op jit(solution)/shard_map/all_to_all | solution.py:102
  715.5 8.0 %all-to-all-start = ((f32[8,32,1]{1,2,0:T(1,128)}), f32[8,32,1]{1,2,0:T(1,128)S(1)}, u32[]{:S(2)}, u32[]{:S(2)}) async-start(f32[8,32,1]{1,2,0:T(1,128)} %bitcast.9), calls=%async_computation.1 | async-start | bytes 8192 | tf_op jit(solution)/shard_map/all_to_all | solution.py:103
Sparse Core Ops, SparseCore 0:
  32.3 34.1 reduce-scatter.1
  93.7 34.7 reduce-scatter.1
  155.7 34.7 reduce-scatter.1
  217.8 34.7 reduce-scatter.1
  279.8 34.7 reduce-scatter.1
  341.8 34.7 reduce-scatter.1
  403.8 34.7 reduce-scatter.1
  465.8 34.7 reduce-scatter.1
  527.8 34.7 reduce-scatter.1
  589.8 34.7 reduce-scatter.1
  651.8 34.7 reduce-scatter.1
where the time goes:
time: 748 us; the launch traced here: 746 us
  waiting for transfers between devices  401 us (54%)
  blocking collectives  131 us (18%)
  matrix products  104 us (14%)
  starting transfers between devices  44 us (6%)
  other arithmetic  23.4 us (3%)
  loops' own time  15.5 us (2%)
  between operations  14.6 us (2%)
  local copies, waits for them, and re-layouts  12.5 us (2%)
    reduce_scatter x11, waiting for transfers between devices, layer_split(): lax.psum_scatter(jnp.dot(hidden, w_down[layer], preferred_element_type=jn...  376 us
    all_gather x11, blocking collectives, layer_split(): piece = lax.all_gather(normed, 'rows', axis=0, tiled=True)  106 us
    dot_general x11, matrix products, layer_split(): jnp.dot(hidden, w_down[layer], preferred_element_type=jnp.float32)  69 us
    ppermute x11, starting transfers between devices, shifted(): lax.ppermute(value, axis, [(source, source + steps) for source in range(f...  37.3 us
    dot_general x11, matrix products, layer_split(): gate = jnp.dot(piece, w_gate[layer], preferred_element_type=jnp.float32)  33.3 us
    ppermute x11, waiting for transfers between devices, shifted(): lax.ppermute(value, axis, [(source, source + steps) for source in range(f...  19 us
    another operation x1, loops' own time, on_device(): lax.scan(tick, (start_state, start_rows), jnp.arange(MICRO + sections - 1))  15.5 us
  transfers between devices with their start and end apart: 24, of which 24 were waited for; matrix products, arithmetic and copies ran while one was open for 0% of the time, Pallas kernels for 0%

commit v1 on v0

v1 whole, which is shorter than its diff:
```python
import functools

import jax
import jax.numpy as jnp
from jax import lax
from jax.experimental import pallas as pl
from jax.experimental.pallas import tpu as pltpu
from jax.sharding import PartitionSpec as P

MICRO = 8
MESH = pl.DeviceIdType.MESH
LANES = 128


def chunks(total, size):
    return [(at, min(size, total - at)) for at in range(0, total, size)]


def remote(src, dst, send_sem, recv_sem, where):
    return pltpu.make_async_remote_copy(
        src_ref=src, dst_ref=dst, send_sem=send_sem, recv_sem=recv_sem,
        device_id=where, device_id_type=MESH,
    )


def kernel(
    sections, groups,
    features, ages, age_table, returns, target, gain, w_gate, w_up, w_down,
    final_gain, head, old,
    rewards_out, weights_out,
    wg, wu, wd, x_in, x_out, gathered, hidden, part, part_in, paired, paired_in,
    reward_cols, marks, marks_wide, result, prio_wide, refreshed, sums,
    w_sem,
    ag_send, ag_recv, fw_send, fw_recv, pr_send, pr_recv, rs_send, rs_recv, z_send, z_recv,
    mk_send, mk_recv, up_send, up_recv, rw_send, rw_recv, sm_send, sm_recv,
):
    sec = lax.axis_index("section")
    me = lax.axis_index("rows")
    chips = groups // 2
    chip, core = me // 2, lax.rem(me, 2)
    other = 1 - core
    sibling = chip * 2 + other
    block, width = x_in.shape[1], x_in.shape[2]
    rows = x_in.shape[0] * block
    ff = hidden.shape[1]
    last = sections - 1

    loads = [
        pltpu.make_async_copy(w_gate, wg, w_sem.at[0]),
        pltpu.make_async_copy(w_up, wu, w_sem.at[1]),
        pltpu.make_async_copy(w_down, wd, w_sem.at[2]),
    ]
    for load in loads:
        load.start()

    barrier = pltpu.get_barrier_semaphore()
    for j in range(1, groups):
        pl.semaphore_signal(barrier, inc=1, device_id={"rows": lax.rem(me + j, groups)}, device_id_type=MESH)
    for j in range(1, sections):
        pl.semaphore_signal(barrier, inc=1, device_id={"section": lax.rem(sec + j, sections)}, device_id_type=MESH)

    marks[me] = target[...]

    @pl.when(sec == 0)
    def _():
        tall = jnp.transpose(jnp.broadcast_to(ages[...].astype(jnp.float32), (LANES, rows)))
        buckets = age_table.shape[0]
        onehot = (
            tall[:, :buckets] == lax.broadcasted_iota(jnp.int32, (rows, buckets), 1).astype(jnp.float32)
        ).astype(jnp.float32).astype(jnp.bfloat16)
        for at, size in chunks(width, 512):
            entry = features[:, at:at + size].astype(jnp.float32) + jnp.dot(
                onehot, age_table[:, at:at + size], preferred_element_type=jnp.float32
            )
            x_in[:, :, at:at + size] = entry.astype(jnp.bfloat16).reshape(MICRO, block, size)

    pl.semaphore_wait(barrier, groups - 1 + sections - 1)

    def to_group(ref, send, recv, j):
        return remote(ref.at[me], ref.at[me], send.at[j], recv.at[j], {"rows": lax.rem(me + j, groups)})

    def from_group(ref, send, recv, j):
        spot = ref.at[lax.rem(me + groups - j, groups)]
        return remote(spot, spot, send.at[j], recv.at[j], {"rows": lax.rem(me + j, groups)})

    def peer(j):
        return {"rows": lax.rem(chip + j, chips) * 2 + core}

    def ag_copy(m, j, spot):
        block_ref = gathered.at[m, core, spot]
        return remote(block_ref, block_ref, ag_send.at[m, j - 1], ag_recv.at[m, j - 1], peer(j))

    def fw_copy(m, half):
        half_ref = gathered.at[m, half]
        return remote(half_ref, half_ref, fw_send.at[m], fw_recv.at[m], {"rows": sibling})

    def pr_copy(m):
        return remote(part.at[m, other], part_in.at[m], pr_send.at[m], pr_recv.at[m], {"rows": sibling})

    def rs_copy(m, j):
        return remote(
            paired.at[m, lax.rem(chip + j, chips)], paired_in.at[m, j - 1],
            rs_send.at[m, j - 1], rs_recv.at[m, j - 1], peer(j),
        )

    def z_copy(m):
        return remote(x_out.at[m], x_in.at[m], z_send.at[m], z_recv.at[m], {"section": jnp.minimum(sec + 1, last)})

    def z_back(m):
        return remote(x_out.at[m], x_in.at[m], z_send.at[m], z_recv.at[m], {"section": jnp.maximum(sec - 1, 0)})

    def stage_a(m):
        @pl.when(sec > 0)
        def _():
            z_back(m).wait_recv()

        wide = x_in[m].astype(jnp.float32)
        scale = lax.rsqrt(jnp.mean(wide * wide, axis=-1, keepdims=True) + 1e-06)
        gathered[m, core, chip] = (wide * scale * gain[...]).astype(jnp.bfloat16)
        for j in range(1, chips):
            ag_copy(m, j, chip).start()

    def stage_f(m):
        for j in range(1, chips):
            ag_copy(m, j, lax.rem(chip + chips - j, chips)).wait_recv()
        fw_copy(m, core).start()

    def stage_b(m):
        fw_copy(m, other).wait_recv()
        piece = gathered[m].reshape(groups * block, width)
        for at, size in chunks(ff, 256):
            gate = jnp.dot(piece, wg[:, at:at + size], preferred_element_type=jnp.float32)
            upper = jnp.dot(piece, wu[:, at:at + size], preferred_element_type=jnp.float32)
            hidden[:, at:at + size] = (gate / (1.0 + jnp.exp(-gate)) * upper).astype(jnp.bfloat16)
        units = hidden[...]
        for at, size in chunks(width, 256):
            down = jnp.dot(units, wd[:, at:at + size], preferred_element_type=jnp.float32)
            part[m, :, :, :, at:at + size] = down.astype(jnp.bfloat16).reshape(2, chips, block, size)
        pr_copy(m).start()

    def stage_r(m):
        pr_copy(m).wait_recv()
        both = part[m, core].astype(jnp.float32) + part_in[m].astype(jnp.float32)
        paired[m] = both.astype(jnp.bfloat16)
        for j in range(1, chips):
            rs_copy(m, j).start()

    def stage_c(m):
        total = x_in[m].astype(jnp.float32) + paired[m, chip].astype(jnp.float32)
        for j in range(1, chips):
            rs_copy(m, j).wait_recv()
            total = total + paired_in[m, j - 1].astype(jnp.float32)
        state = total.astype(jnp.bfloat16)
        x_out[m] = state

        @pl.when(sec < last)
        def _():
            z_copy(m).start()

        @pl.when(sec == last)
        def _():
            wide = state.astype(jnp.float32)
            scale = lax.rsqrt(jnp.mean(wide * wide, axis=-1, keepdims=True) + 1e-06)
            value = jnp.sum(wide * scale * final_gain[...] * head[...], axis=-1, keepdims=True)
            reward_cols[m] = jnp.broadcast_to(value, (block, LANES))

    stage_a(0)
    for j in range(1, groups):
        to_group(marks, mk_send, mk_recv, j).start()
    stage_f(0)
    for load in loads:
        load.wait()

    def step(t, carry):
        @pl.when(t + 1 < MICRO)
        def _():
            stage_a(t + 1)

        @pl.when(t < MICRO)
        def _():
            stage_b(t)

        @pl.when(t >= 1)
        def _():
            stage_c(t - 1)

        @pl.when(t < MICRO)
        def _():
            stage_r(t)

        @pl.when(t + 1 < MICRO)
        def _():
            stage_f(t + 1)

        return carry

    lax.fori_loop(0, MICRO + 1, step, 0)

    for j in range(1, groups):
        from_group(marks, mk_send, mk_recv, j).wait_recv()
    for r in range(groups):
        marks_wide[r] = jnp.transpose(jnp.broadcast_to(marks[r], (LANES, rows)))

    def up_copy(j):
        return remote(result.at[me], result.at[me], up_send.at[j - 1], up_recv.at[0], {"section": last - j})

    @pl.when(sec == last)
    def _():
        square = reward_cols[...].reshape(rows, LANES)
        on_line = lax.broadcasted_iota(jnp.int32, (rows, rows), 0) == lax.broadcasted_iota(jnp.int32, (rows, rows), 1)
        row = jnp.sum(jnp.where(on_line, square, 0.0), axis=0, keepdims=True)
        priority = jnp.exp(0.6 * jnp.log(jnp.abs(row - returns[...]) + 0.05))
        result[me, 0:1] = row
        result[me, 1:2] = priority
        for j in range(1, sections):
            up_copy(j).start()

    @pl.when(sec < last)
    def _():
        up_copy(1).wait_recv()

    for j in range(1, groups):
        to_group(result, rw_send, rw_recv, j).start()

    mine = result[me, 0:1]
    share = rows // sections
    picked = mine[:, 0:share]
    for s in range(1, sections):
        picked = jnp.where(sec == s, mine[:, s * share:(s + 1) * share], picked)
    rewards_out[...] = picked

    for j in range(1, groups):
        from_group(result, rw_send, rw_recv, j).wait_recv()
    for r in range(groups):
        prio_wide[r] = jnp.transpose(jnp.broadcast_to(result[r, 1:2], (LANES, rows)))

    lines = old.shape[0]
    table = lines * LANES
    batch = 4
    lane = lax.broadcasted_iota(jnp.int32, (1, LANES), 1).astype(jnp.float32)

    def match(g, carry):
        first = (me * table + g * (batch * LANES)).astype(jnp.float32)
        names = [first + (q * LANES) + lane for q in range(batch)]

        def one(r, best):
            best = list(best)
            for i in range(0, rows, 8):
                mark = marks_wide[r, i:i + 8, :]
                prio = prio_wide[r, i:i + 8, :]
                for q in range(batch):
                    best[q] = jnp.maximum(best[q], jnp.where(mark == names[q], prio, 0.0))
            return tuple(best)

        best = lax.fori_loop(0, groups, one, tuple(jnp.zeros((8, LANES), jnp.float32) for _ in range(batch)))
        for q in range(batch):
            top = jnp.max(best[q], axis=0, keepdims=True)
            at = pl.ds(g * batch + q, 1)
            refreshed[at, :] = jnp.where(top > 0.0, top, old[at, :])
        return carry

    lax.fori_loop(0, lines // batch, match, 0)
    subtotal = jnp.sum(jnp.sum(refreshed[...], axis=0, keepdims=True), axis=1, keepdims=True)
    sums[me] = jnp.broadcast_to(subtotal, (1, LANES))
    for j in range(1, groups):
        to_group(sums, sm_send, sm_recv, j).start()

    for m in range(MICRO):
        for j in range(1, chips):
            ag_copy(m, j, chip).wait_send()
            rs_copy(m, j).wait_send()
        fw_copy(m, core).wait_send()
        pr_copy(m).wait_send()

    @pl.when(sec < last)
    def _():
        for m in range(MICRO):
            z_copy(m).wait_send()

    @pl.when(sec == last)
    def _():
        for j in range(1, sections):
            up_copy(j).wait_send()

    for j in range(1, groups):
        to_group(marks, mk_send, mk_recv, j).wait_send()
        to_group(result, rw_send, rw_recv, j).wait_send()

    for j in range(1, groups):
        from_group(sums, sm_send, sm_recv, j).wait_recv()
    total = sums[0]
    for r in range(1, groups):
        total = total + sums[r]
    tall = lines // sections
    weights_out[...] = refreshed[pl.ds(sec * tall, tall), :] * (table * groups / total)
    for j in range(1, groups):
        to_group(sums, sm_send, sm_recv, j).wait_send()


def on_device(
    features, ages, age_table, returns, owners, slots, norm_gain,
    w_gate, w_up, w_down, final_gain, reward_head, old_priority,
):
    sections, groups = lax.axis_size("section"), lax.axis_size("rows")
    rows, width = features.shape
    block = rows // MICRO
    chips = groups // 2
    ff = w_gate.shape[2]
    table = old_priority.shape[0]
    lines = table // LANES
    target = (owners[:, 0] * table + slots).astype(jnp.float32).reshape(1, rows)
    vmem = pl.BlockSpec(memory_space=pltpu.VMEM)
    far = pl.BlockSpec(memory_space=pl.ANY)
    bf16, f32, dma = jnp.bfloat16, jnp.float32, pltpu.SemaphoreType.DMA
    rewards, weights = pl.pallas_call(
        functools.partial(kernel, sections, groups),
        out_shape=(
            jax.ShapeDtypeStruct((1, rows // sections), f32),
            jax.ShapeDtypeStruct((lines // sections, LANES), f32),
        ),
        in_specs=[vmem] * 6 + [far] * 3 + [vmem] * 3,
        out_specs=(vmem, vmem),
        scratch_shapes=[
            pltpu.VMEM((width, ff), bf16),
            pltpu.VMEM((width, ff), bf16),
            pltpu.VMEM((ff, width), bf16),
            pltpu.VMEM((MICRO, block, width), bf16),
            pltpu.VMEM((MICRO, block, width), bf16),
            pltpu.VMEM((MICRO, 2, chips, block, width), bf16),
            pltpu.VMEM((groups * block, ff), bf16),
            pltpu.VMEM((MICRO, 2, chips, block, width), bf16),
            pltpu.VMEM((MICRO, chips, block, width), bf16),
            pltpu.VMEM((MICRO, chips, block, width), bf16),
            pltpu.VMEM((MICRO, chips - 1, block, width), bf16),
            pltpu.VMEM((MICRO, block, LANES), f32),
            pltpu.VMEM((groups, 1, rows), f32),
            pltpu.VMEM((groups, rows, LANES), f32),
            pltpu.VMEM((groups, 2, rows), f32),
            pltpu.VMEM((groups, rows, LANES), f32),
            pltpu.VMEM((lines, LANES), f32),
            pltpu.VMEM((groups, 1, LANES), f32),
            dma((3,)),
            dma((MICRO, chips - 1)), dma((MICRO, chips - 1)),
            dma((MICRO,)), dma((MICRO,)),
            dma((MICRO,)), dma((MICRO,)),
            dma((MICRO, chips - 1)), dma((MICRO, chips - 1)),
            dma((MICRO,)), dma((MICRO,)),
            dma((groups,)), dma((groups,)),
            dma((sections - 1,)), dma((1,)),
            dma((groups,)), dma((groups,)),
            dma((groups,)), dma((groups,)),
        ],
        compiler_params=pltpu.CompilerParams(
            collective_id=0, has_side_effects=True, vmem_limit_bytes=56 * 1024 * 1024
        ),
        name="refresh",
    )(
        features, ages.reshape(1, rows), age_table, returns.reshape(1, rows), target,
        norm_gain, w_gate[0], w_up[0], w_down[0],
        final_gain.reshape(1, width), reward_head.reshape(1, width),
        old_priority.reshape(lines, LANES),
    )
    return rewards.reshape(-1), weights.reshape(-1)


def solution(mesh):
    placed = (
        P("rows", None),
        P("rows"),
        P(),
        P("rows"),
        P("rows", None),
        P("rows"),
        P("section", None),
        P("section", None, "rows"),
        P("section", None, "rows"),
        P("section", "rows", None),
        P(),
        P(),
        P("rows"),
    )
    return jax.shard_map(
        on_device,
        mesh=mesh,
        in_specs=placed,
        out_specs=(P(("rows", "section")), P(("rows", "section"))),
        check_vma=False,
    )
```

time: 748 us -> 135 us (0.18)
  waiting for transfers between devices: 401 us -> 0 us
  blocking collectives: 131 us -> 0 us
  Pallas kernels: 0 us -> 118 us
  matrix products: 104 us -> 0 us
  starting transfers between devices: 44 us -> 0 us
  other arithmetic: 23.4 us -> 1.19 us
  loops' own time: 15.5 us -> 0 us
  between operations: 14.6 us -> 0.64 us
    reduce_scatter x11 -> x0, waiting for transfers between devices: 376 us -> none  [layer_split(): lax.psum_scatter(jnp.dot(hidden, w_down[layer], preferred_element_type=jn...]
    pallas_call x0 -> x1, Pallas kernels: none -> 118 us  [on_device(): pl.pallas_call(functools.partial(kernel, sections, groups), out_shape=(ja...]
    all_gather x11 -> x0, blocking collectives: 106 us -> none  [layer_split(): piece = lax.all_gather(normed, 'rows', axis=0, tiled=True)]
    dot_general x23 -> x0, matrix products: 104 us -> none  [the longest x11 69 us: layer_split(): jnp.dot(hidden, w_down[layer], preferred_element_type=jnp.float32)]
    ppermute x11 -> x0, starting transfers between devices: 37.3 us -> none  [shifted(): lax.ppermute(value, axis, [(source, source + steps) for source in range(f...]
    psum x2 -> x0, blocking collectives: 25 us -> none  [the longest x1 12.5 us: spread(): return lax.psum(kept, axis)]
    ppermute x11 -> x0, waiting for transfers between devices: 19 us -> none  [shifted(): lax.ppermute(value, axis, [(source, source + steps) for source in range(f...]
    another operation x1 -> x0, loops' own time: 15.5 us -> none  [on_device(): lax.scan(tick, (start_state, start_rows), jnp.arange(MICRO + sections - 1))]
  transfers between devices with their start and end apart: 24 -> 0, of which waited for: 24 -> 0; matrix products, arithmetic and copies ran while one was open for 0% -> 0% of each run, Pallas kernels for 0% -> 0%
where the time goes in v1:
time: 135 us; the launch traced here: 134 us
  Pallas kernels  118 us (87%)
  local copies, waits for them, and re-layouts  14.8 us (11%)
    pallas_call x1, Pallas kernels, on_device(): pl.pallas_call(functools.partial(kernel, sections, groups), out_shape=(ja...  118 us
    unnamed x6, local copies, waits for them, and re-layouts  12.2 us

profile of v1, /device:TPU:0, one launch (start us, length us, event | category | flops | bytes accessed | tf_op | source)
XLA Modules:
  0.0 134.4 jit_solution(4553755134144997849)
XLA Ops:
  0.6 1.2 fusion.1.target
  1.8 1.3 reshape.33.final_gain
  3.1 1.3 reshape.34.head
  4.4 0.0 copy-start
  4.4 5.9 %copy.15 = bf16[1,1536,1120]{2,1,0:T(8,128)(2,1)} copy(bf16[1,1536,1120]{1,2,0:T(8,128)(2,1)} %param.20) | data formatting | bytes 6881280 | tf_op args[7]
  10.3 0.0 copy-done
  10.3 3.8 %copy.16 = bf16[1,1536,1120]{2,1,0:T(8,128)(2,1)} copy(bf16[1,1536,1120]{1,2,0:T(8,128)(2,1)S(1)} %copy-done) | data formatting | bytes 6881280 | tf_op args[8]
  14.1 117.8 %refresh.1 = (f32[1,32]{1,0:T(1,128)}, f32[8,128]{1,0:T(8,128)}) custom-call(bf16[128,1536]{1,0:T(8,128)(2,1)} %features.1, s32[1,128]{1,0:T(1,128)} %bitcast.21, bf16[16,1536]{1,0:T(8,128)(2,1)} %age_table.1, f32[1,128]{1,0:T(1,128)} %bitcast.22, f32[1,128]{1,0:T(1,128)} %fusion.1.target, f32[1,1536]{1,0:T(1,128)} %gain.1, bf16[1536,1120]{1,0:T(8,128)(2,1)} %bitcast.16, ...), custom_call_target="tpu_custom_call" | custom-call | tf_op jit(solution)/shard_map/refresh/pallas_call | solution.py:315
  131.9 1.2 copy.19
  133.1 1.3 copy.20
Async XLA Ops:
  4.4 5.9 %copy-start = (bf16[1,1536,1120]{1,2,0:T(8,128)(2,1)S(1)}, bf16[1,1536,1120]{1,2,0:T(8,128)(2,1)}, u32[]{:S(2)}) copy-start(bf16[1,1536,1120]{1,2,0:T(8,128)(2,1)} %param.21) | copy-start | bytes 10321924

commit v2 on v1

--- a/solution.py
+++ b/solution.py
@@ -16,6 +16,15 @@
     return [(at, min(size, total - at)) for at in range(0, total, size)]
 
 
+def flipped(index, mask):
+    moved, bit = index, 1
+    while bit <= mask:
+        if mask & bit:
+            moved = moved + bit * (1 - 2 * lax.rem(index // bit, 2))
+        bit *= 2
+    return moved
+
+
 def remote(src, dst, send_sem, recv_sem, where):
     return pltpu.make_async_remote_copy(
         src_ref=src, dst_ref=dst, send_sem=send_sem, recv_sem=recv_sem,
@@ -25,11 +34,11 @@
 
 def kernel(
     sections, groups,
-    features, ages, age_table, returns, target, gain, w_gate, w_up, w_down,
+    features, ages, age_table, returns, owners, slots, gain, w_gate, w_up, w_down,
     final_gain, head, old,
     rewards_out, weights_out,
-    wg, wu, wd, x_in, x_out, gathered, hidden, part, part_in, paired, paired_in,
-    reward_cols, marks, marks_wide, result, prio_wide, refreshed, sums,
+    wg, wu, wd, wg_up, wu_up, x_in, x_out, gathered, hidden, part, part_in, paired, paired_in,
+    final_row, reward_cols, marks, marks_wide, result, prio_wide, refreshed, sums,
     w_sem,
     ag_send, ag_recv, fw_send, fw_recv, pr_send, pr_recv, rs_send, rs_recv, z_send, z_recv,
     mk_send, mk_recv, up_send, up_recv, rw_send, rw_recv, sm_send, sm_recv,
@@ -40,6 +49,7 @@
     chip, core = me // 2, lax.rem(me, 2)
     other = 1 - core
     sibling = chip * 2 + other
+    far_first = sorted(range(1, chips), key=lambda j: (-j.bit_count(), j))
     block, width = x_in.shape[1], x_in.shape[2]
     rows = x_in.shape[0] * block
     ff = hidden.shape[1]
@@ -50,8 +60,8 @@
         pltpu.make_async_copy(w_up, wu, w_sem.at[1]),
         pltpu.make_async_copy(w_down, wd, w_sem.at[2]),
     ]
-    for load in loads:
-        load.start()
+    loads[0].start()
+    loads[1].start()
 
     barrier = pltpu.get_barrier_semaphore()
     for j in range(1, groups):
@@ -59,7 +69,11 @@
     for j in range(1, sections):
         pl.semaphore_signal(barrier, inc=1, device_id={"section": lax.rem(sec + j, sections)}, device_id_type=MESH)
 
-    marks[me] = target[...]
+    marks[me] = (owners[...] * (old.shape[0] * LANES) + slots[...]).astype(jnp.float32)
+
+    for i in range(final_gain.shape[0]):
+        final_row[0:1, i * LANES:(i + 1) * LANES] = final_gain[i:i + 1, :]
+        final_row[1:2, i * LANES:(i + 1) * LANES] = head[i:i + 1, :]
 
     @pl.when(sec == 0)
     def _():
@@ -84,7 +98,7 @@
         return remote(spot, spot, send.at[j], recv.at[j], {"rows": lax.rem(me + j, groups)})
 
     def peer(j):
-        return {"rows": lax.rem(chip + j, chips) * 2 + core}
+        return {"rows": flipped(chip, j) * 2 + core}
 
     def ag_copy(m, j, spot):
         block_ref = gathered.at[m, core, spot]
@@ -99,7 +113,7 @@
 
     def rs_copy(m, j):
         return remote(
-            paired.at[m, lax.rem(chip + j, chips)], paired_in.at[m, j - 1],
+            paired.at[m, flipped(chip, j)], paired_in.at[m, j - 1],
             rs_send.at[m, j - 1], rs_recv.at[m, j - 1], peer(j),
         )
 
@@ -117,20 +131,20 @@
         wide = x_in[m].astype(jnp.float32)
         scale = lax.rsqrt(jnp.mean(wide * wide, axis=-1, keepdims=True) + 1e-06)
         gathered[m, core, chip] = (wide * scale * gain[...]).astype(jnp.bfloat16)
-        for j in range(1, chips):
+        for j in far_first:
             ag_copy(m, j, chip).start()
 
     def stage_f(m):
-        for j in range(1, chips):
-            ag_copy(m, j, lax.rem(chip + chips - j, chips)).wait_recv()
+        for j in far_first:
+            ag_copy(m, j, flipped(chip, j)).wait_recv()
         fw_copy(m, core).start()
 
     def stage_b(m):
         fw_copy(m, other).wait_recv()
         piece = gathered[m].reshape(groups * block, width)
         for at, size in chunks(ff, 256):
-            gate = jnp.dot(piece, wg[:, at:at + size], preferred_element_type=jnp.float32)
-            upper = jnp.dot(piece, wu[:, at:at + size], preferred_element_type=jnp.float32)
+            gate = jnp.dot(piece, wg_up[:, at:at + size], preferred_element_type=jnp.float32)
+            upper = jnp.dot(piece, wu_up[:, at:at + size], preferred_element_type=jnp.float32)
             hidden[:, at:at + size] = (gate / (1.0 + jnp.exp(-gate)) * upper).astype(jnp.bfloat16)
         units = hidden[...]
         for at, size in chunks(width, 256):
@@ -142,12 +156,12 @@
         pr_copy(m).wait_recv()
         both = part[m, core].astype(jnp.float32) + part_in[m].astype(jnp.float32)
         paired[m] = both.astype(jnp.bfloat16)
-        for j in range(1, chips):
+        for j in far_first:
             rs_copy(m, j).start()
 
     def stage_c(m):
         total = x_in[m].astype(jnp.float32) + paired[m, chip].astype(jnp.float32)
-        for j in range(1, chips):
+        for j in far_first:
             rs_copy(m, j).wait_recv()
             total = total + paired_in[m, j - 1].astype(jnp.float32)
         state = total.astype(jnp.bfloat16)
@@ -161,15 +175,20 @@
         def _():
             wide = state.astype(jnp.float32)
             scale = lax.rsqrt(jnp.mean(wide * wide, axis=-1, keepdims=True) + 1e-06)
-            value = jnp.sum(wide * scale * final_gain[...] * head[...], axis=-1, keepdims=True)
+            value = jnp.sum(wide * scale * final_row[0:1] * final_row[1:2], axis=-1, keepdims=True)
             reward_cols[m] = jnp.broadcast_to(value, (block, LANES))
 
     stage_a(0)
     for j in range(1, groups):
         to_group(marks, mk_send, mk_recv, j).start()
+    for load, flat, tall in ((loads[0], wg, wg_up), (loads[1], wu, wu_up)):
+        load.wait()
+        if load is loads[0]:
+            loads[2].start()
+        for at, size in chunks(ff, 256):
+            tall[:, at:at + size] = jnp.transpose(flat[at:at + size, :])
     stage_f(0)
-    for load in loads:
-        load.wait()
+    loads[2].wait()
 
     def step(t, carry):
         @pl.when(t + 1 < MICRO)
@@ -266,7 +285,7 @@
         to_group(sums, sm_send, sm_recv, j).start()
 
     for m in range(MICRO):
-        for j in range(1, chips):
+        for j in far_first:
             ag_copy(m, j, chip).wait_send()
             rs_copy(m, j).wait_send()
         fw_copy(m, core).wait_send()
@@ -295,6 +314,11 @@
     weights_out[...] = refreshed[pl.ds(sec * tall, tall), :] * (table * groups / total)
     for j in range(1, groups):
         to_group(sums, sm_send, sm_recv, j).wait_send()
+
+
+def handed(rewards, weights, rewards_out, weights_out):
+    rewards_out[...] = rewards[...]
+    weights_out[...] = weights[...]
 
 
 def on_device(
@@ -308,7 +332,6 @@
     ff = w_gate.shape[2]
     table = old_priority.shape[0]
     lines = table // LANES
-    target = (owners[:, 0] * table + slots).astype(jnp.float32).reshape(1, rows)
     vmem = pl.BlockSpec(memory_space=pltpu.VMEM)
     far = pl.BlockSpec(memory_space=pl.ANY)
     bf16, f32, dma = jnp.bfloat16, jnp.float32, pltpu.SemaphoreType.DMA
@@ -318,12 +341,14 @@
             jax.ShapeDtypeStruct((1, rows // sections), f32),
             jax.ShapeDtypeStruct((lines // sections, LANES), f32),
         ),
-        in_specs=[vmem] * 6 + [far] * 3 + [vmem] * 3,
+        in_specs=[vmem] * 7 + [far] * 3 + [vmem] * 3,
         out_specs=(vmem, vmem),
         scratch_shapes=[
+            pltpu.VMEM((ff, width), bf16),
+            pltpu.VMEM((ff, width), bf16),
+            pltpu.VMEM((ff, width), bf16),
             pltpu.VMEM((width, ff), bf16),
             pltpu.VMEM((width, ff), bf16),
-            pltpu.VMEM((ff, width), bf16),
             pltpu.VMEM((MICRO, block, width), bf16),
             pltpu.VMEM((MICRO, block, width), bf16),
             pltpu.VMEM((MICRO, 2, chips, block, width), bf16),
@@ -332,6 +357,7 @@
             pltpu.VMEM((MICRO, chips, block, width), bf16),
             pltpu.VMEM((MICRO, chips, block, width), bf16),
             pltpu.VMEM((MICRO, chips - 1, block, width), bf16),
+            pltpu.VMEM((2, width), f32),
             pltpu.VMEM((MICRO, block, LANES), f32),
             pltpu.VMEM((groups, 1, rows), f32),
             pltpu.VMEM((groups, rows, LANES), f32),
@@ -355,11 +381,16 @@
         ),
         name="refresh",
     )(
-        features, ages.reshape(1, rows), age_table, returns.reshape(1, rows), target,
-        norm_gain, w_gate[0], w_up[0], w_down[0],
-        final_gain.reshape(1, width), reward_head.reshape(1, width),
+        features, ages.reshape(1, rows), age_table, returns.reshape(1, rows),
+        owners.reshape(1, rows), slots.reshape(1, rows),
+        norm_gain, w_gate[0].T, w_up[0].T, w_down[0],
+        final_gain.reshape(-1, LANES), reward_head.reshape(-1, LANES),
         old_priority.reshape(lines, LANES),
     )
+    rewards, weights = pl.pallas_call(
+        handed, out_shape=tuple(jax.ShapeDtypeStruct(each.shape, f32) for each in (rewards, weights)),
+        in_specs=[vmem, vmem], out_specs=(vmem, vmem), name="handed",
+    )(rewards, weights)
     return rewards.reshape(-1), weights.reshape(-1)
 
 

time: 135 us -> 118 us (0.87)
  local copies, waits for them, and re-layouts: 14.8 us -> 0 us
    unnamed x6 -> x0, local copies, waits for them, and re-layouts: 12.2 us -> none
    reshape x2 -> x0, local copies, waits for them, and re-layouts: 2.59 us -> none  [the longest x1 1.3 us: on_device(): final_gain.reshape(1, width)]
    pallas_call x1, Pallas kernels: 118 us -> 116 us  [on_device(): pl.pallas_call(functools.partial(kernel, sections, groups), out_shape=(ja...]
where the time goes in v2:
time: 118 us
  Pallas kernels  117 us (99%)
    pallas_call x1, Pallas kernels, on_device(): pl.pallas_call(functools.partial(kernel, sections, groups), out_shape=(ja...  116 us

profile of v2, /device:TPU:0, one launch (start us, length us, event | category | flops | bytes accessed | tf_op | source)
XLA Modules:
  0.0 118.0 jit_solution(5106703537353422182)
XLA Ops:
  0.6 116.1 %refresh.1 = (f32[1,32]{1,0:T(1,128)}, f32[8,128]{1,0:T(8,128)}) custom-call(bf16[128,1536]{1,0:T(8,128)(2,1)} %features.1, s32[1,128]{1,0:T(1,128)} %bitcast.22, bf16[16,1536]{1,0:T(8,128)(2,1)} %age_table.1, f32[1,128]{1,0:T(1,128)} %bitcast.23, s32[1,128]{1,0:T(1,128)} %bitcast.24, s32[1,128]{1,0:T(1,128)} %bitcast.25, f32[1,1536]{1,0:T(1,128)} %gain.1, ...), custom_call_target="tpu_custom_call" | custom-call | tf_op jit(solution)/shard_map/refresh/pallas_call | solution.py:338
  116.7 1.3 %handed.1 = (f32[1,32]{1,0:T(1,128)}, f32[8,128]{1,0:T(8,128)}) custom-call(f32[1,32]{1,0:T(1,128)} %get-tuple-element.6.rewards, f32[8,128]{1,0:T(8,128)} %get-tuple-element.7.weights), custom_call_target="tpu_custom_call" | custom-call | tf_op jit(solution)/shard_map/handed/pallas_call | solution.py:390
